TPU v7x, 32 devices: a whole 2x2x4 slice. The times are simulated.
32 devices in a mesh: tm: 2 (over y), space: 4 (over z), member: 4 (over x, core).
Axes of the slice: x: 2, y: 2, z: 4, core: 2. Of those that a mesh axis runs over, the one named last changes fastest.
Arguments:
- obs_anom: bfloat16 [6, 2, 8, 256, 1024], P('tm', None, 'space', 'member'), may hold values from -0.59375 to 0.59375
- obs_prec: bfloat16 [6, 2, 8, 1024], P('tm', None, 'space'), may hold values from 0.29882812 to 3
- innov: bfloat16 [6, 2, 8, 1024], P('tm', None, 'space'), may hold values from -6 to 6
- obs_column: int32 [6, 2, 8, 1024], P('tm', None, 'space'), may hold values from 0 to 127
- cutoff: int32 [2, 8], replicated, may hold values from 1 to 2
- inv_root: float32 [2, 8, 256, 256], P('tm', 'space'), may hold values from -0.12 to 0.12
- state_anom: bfloat16 [2, 8, 256, 32, 128], P('tm', 'space', None, 'member'), may hold values from -6 to 6
- state_mean: float32 [2, 8, 32, 128], P('tm', 'space', 'member'), may hold values from -6 to 6
Outputs:
- analysis: bfloat16 [2, 8, 256, 32, 128], P('tm', 'space', None, 'member')
All inputs are finite; a program needn't handle non-finite values.
Results may differ from a plain program's by a relative error of at most 0.0062.
Values may be sent and summed in bfloat16 or wider, within the bound.
A program may use at most 64 MiB of HBM per device.

v0:
```python
import math

import jax
import jax.numpy as jnp
from jax import lax
from jax.sharding import PartitionSpec as P

K = 256
HALO = 2
NEWTON = 2


def with_halo(cells, sides, width):
    for axis, dim in sides:
        count = lax.axis_size(axis)
        head = lax.slice_in_dim(cells, 0, width, axis=dim)
        tail = lax.slice_in_dim(cells, cells.shape[dim] - width, cells.shape[dim], axis=dim)
        cells = jnp.concatenate(
            [
                lax.ppermute(tail, axis, [(i, (i + 1) % count) for i in range(count)]),
                cells,
                lax.ppermute(head, axis, [((i + 1) % count, i) for i in range(count)]),
            ],
            axis=dim,
        )
    return cells


def taper_weight(distance, reach_now, columns):
    scaled_reach = (reach_now + 0.5) * columns
    relative = distance / scaled_reach
    return jnp.square(jnp.maximum(1.0 - relative * relative, 0.0))


def tile_cutoffs(cutoff, first_tile, how_many):
    flattened = cutoff.reshape(-1)
    cycle_size = flattened.shape[0]
    wanted = (first_tile + jnp.arange(how_many, dtype=jnp.int32) + cycle_size) % cycle_size
    matches = wanted[:, None] == jnp.arange(cycle_size, dtype=jnp.int32)[None, :]
    return jnp.sum(jnp.where(matches, flattened[None, :], 0), axis=1).astype(jnp.float32)


def spread_sums(relaid, reaches, shifts, columns):
    members = relaid.shape[2] - 3
    tile_count = relaid.shape[1]
    window_len = shifts.shape[0]
    extended = tile_count + window_len - 1
    start_gram = jnp.zeros((extended, members, members), jnp.float32)
    start_proj = jnp.zeros((extended, members), jnp.float32)

    def add_tile(tile_index, carry):
        gram_sums, proj_sums = carry
        obs_slab = lax.dynamic_index_in_dim(relaid, tile_index, 1, keepdims=False)
        anomaly = obs_slab[:, :members]
        precision = obs_slab[:, members].astype(jnp.float32)
        innovation = obs_slab[:, members + 1].astype(jnp.float32)
        placing = obs_slab[:, members + 2].astype(jnp.float32)
        reach_now = lax.dynamic_slice_in_dim(reaches, tile_index, window_len, 0)
        distance = shifts[:, None, None] * columns + placing[None]
        coeffs = taper_weight(distance, reach_now[:, None, None], columns) * precision[None]
        scaled = (anomaly[None] * coeffs[:, :, None, :]).astype(jnp.bfloat16)
        weighted = (coeffs * innovation[None]).astype(jnp.bfloat16)
        gram_part = jnp.einsum("wsko,slo->wkl", scaled, anomaly, preferred_element_type=jnp.float32)
        proj_part = jnp.einsum("sko,wso->wk", anomaly, weighted, preferred_element_type=jnp.float32)
        gram_sums = lax.dynamic_update_slice_in_dim(
            gram_sums,
            lax.dynamic_slice_in_dim(gram_sums, tile_index, window_len, 0) + gram_part,
            tile_index,
            0,
        )
        proj_sums = lax.dynamic_update_slice_in_dim(
            proj_sums,
            lax.dynamic_slice_in_dim(proj_sums, tile_index, window_len, 0) + proj_part,
            tile_index,
            0,
        )
        return (gram_sums, proj_sums)

    return lax.fori_loop(0, tile_count, add_tile, (start_gram, start_proj))


def body(obs_anom, obs_prec, innov, obs_column, cutoff, inv_root, state_anom, state_mean):
    columns = state_anom.shape[-1]
    placing = (obs_column.astype(jnp.float32) + (0.5 - columns / 2)).astype(jnp.bfloat16)
    obs_info = jnp.stack([obs_prec, innov, placing], axis=3)
    quarter = obs_anom.shape[4] // lax.axis_size("member")
    own_part = lax.dynamic_slice_in_dim(obs_info, lax.axis_index("member") * quarter, quarter, 4)
    ensemble = lax.all_to_all(obs_anom, "member", split_axis=4, concat_axis=3, tiled=True)
    combined = jnp.concatenate([ensemble, own_part], axis=3)
    relaid = lax.all_to_all(combined, "tm", split_axis=1, concat_axis=0, tiled=True)[:, 0]
    tile_count = relaid.shape[1]
    first_tile = (
        lax.axis_index("tm") * lax.axis_size("space") + lax.axis_index("space")
    ) * tile_count
    window_len = 2 * HALO + 1
    reaches = tile_cutoffs(cutoff, first_tile - HALO, tile_count + 2 * HALO)
    shifts = (HALO - jnp.arange(window_len, dtype=jnp.int32)).astype(jnp.float32)
    ext_gram, ext_proj = spread_sums(relaid, reaches, shifts, columns)
    stacked = jnp.concatenate([ext_gram, ext_proj[:, None, :]], axis=1)
    outgoing = jnp.concatenate([stacked[:HALO], stacked[tile_count + HALO :]], axis=0)
    arrived = with_halo(outgoing, ((("tm", "space"), 0),), HALO)
    owned = stacked[HALO : HALO + tile_count]
    owned = owned.at[:HALO].add(arrived[:HALO])
    owned = owned.at[tile_count - HALO :].add(arrived[3 * HALO :])
    gram_sums = owned[:, :K]
    proj_sums = owned[:, K]
    gram_sums, proj_sums = lax.psum((gram_sums, proj_sums), "member")
    highest = lax.Precision.HIGHEST
    identity = jnp.eye(K, dtype=jnp.float32)
    system = (K - 1.0) * identity + gram_sums
    inv_sqrt = inv_root[0]
    for newton_step in range(NEWTON):
        square = jnp.einsum("tij,tjk->tik", inv_sqrt, inv_sqrt, precision=highest)
        applied = jnp.einsum("tij,tjk->tik", system, square, precision=highest)
        inv_sqrt = 1.5 * inv_sqrt - 0.5 * jnp.einsum(
            "tij,tjk->tik", inv_sqrt, applied, precision=highest
        )
    inner_prod = jnp.einsum("tij,tj->ti", inv_sqrt, proj_sums, precision=highest)
    mean_weight = jnp.einsum("tij,tj->ti", inv_sqrt, inner_prod, precision=highest)
    weights = (mean_weight[:, :, None] + math.sqrt(K - 1) * inv_sqrt).astype(jnp.bfloat16)
    anomalies = state_anom[0].reshape(tile_count, K, -1)
    mean_rows = state_mean[0].reshape(tile_count, 1, -1)
    result = (
        jnp.einsum("tij,tiq->tjq", weights, anomalies, preferred_element_type=jnp.float32)
        + mean_rows
    )
    return result.astype(jnp.bfloat16).reshape(state_anom.shape)


def solution(mesh):
    in_specs = (
        P("tm", None, "space", "member", None),
        P("tm", None, "space", None),
        P("tm", None, "space", None),
        P("tm", None, "space", None),
        P(),
        P("tm", "space", None, None),
        P("tm", "space", None, "member", None),
        P("tm", "space", "member", None),
    )
    out_specs = P("tm", "space", None, "member", None)
    return jax.shard_map(body, mesh=mesh, in_specs=in_specs, out_specs=out_specs, check_vma=False)
```

profile of v0, /device:TPU:0, one launch (start us, length us, event | category | flops | bytes accessed | tf_op | source)
XLA Modules:
  0.0 166.9 jit_solution(3729697214545219223)
XLA Ops:
  6.5 7.3 %copy.73 = bf16[3,2,2,64,1024]{3,0,2,1,4:T(4,128)(2,1)} copy(bf16[3,2,2,64,1024]{4,3,2,1,0:T(8,128)(2,1)} %param.18) | data formatting | bytes 3145728 | tf_op args[0]
  13.9 5.5 %reshape.154 = bf16[4,2,98304]{2,1,0:T(2,128)(2,1)} reshape(bf16[1024,2,2,3,64]{4,3,2,1,0:T(4,128)(2,1)} %bitcast.100) | data formatting | bytes 3145728
  19.4 4.4 %all-to-all-start = ((bf16[4,2,98304]{2,1,0:T(2,128)(2,1)}), bf16[4,2,98304]{2,1,0:T(2,128)(2,1)S(1)}, u32[]{:S(2)}, u32[]{:S(2)}) async-start(bf16[4,2,98304]{2,1,0:T(2,128)(2,1)} %reshape.154), calls=%async_computation | async-start | bytes 3145728 | tf_op jit(solution)/shard_map/all_to_all | solution.py:88
  23.8 0.0 copy-done.4
  23.8 0.0 copy-done.5
  23.8 0.0 copy-done.6
  23.9 19.9 %all-to-all-done = bf16[4,2,98304]{2,1,0:T(2,128)(2,1)S(1)} async-done(((bf16[4,2,98304]{2,1,0:T(2,128)(2,1)}), bf16[4,2,98304]{2,1,0:T(2,128)(2,1)S(1)}, u32[]{:S(2)}, u32[]{:S(2)}) %all-to-all-start) | async-done | bytes 1572896 | tf_op jit(solution)/shard_map/all_to_all | solution.py:88
  43.8 3.8 %reshape.155 = bf16[1024,2,2,3,64]{4,3,2,1,0:T(4,128)(2,1)} reshape(bf16[4,2,98304]{2,1,0:T(2,128)(2,1)S(1)} %all-to-all-done) | data formatting | bytes 3145728
  47.6 9.8 %copy.74 = bf16[3,2,2,4,64,256]{5,2,4,3,0,1:T(2,128)(2,1)S(1)} copy(bf16[3,2,2,4,64,256]{4,0,2,1,5,3:T(4,128)(2,1)} %bitcast.99) | data formatting | bytes 3145728 | tf_op jit(solution)/shard_map/all_to_all | solution.py:88
  57.4 3.2 %pad_maximum_fusion = bf16[3,2,2,259,256]{4,2,3,0,1:T(2,128)(2,1)} fusion(bf16[3,2,2,3,256]{4,2,3,0,1:T(2,128)(2,1)S(1)} %fusion.35, bf16[3,2,2,256,256]{4,2,3,0,1:T(2,128)(2,1)S(1)} %bitcast.102), kind=kLoop, calls=%fused_computation.29 | loop fusion | flops 795648 | bytes 3182592 | tf_op jit(solution)/shard_map/concatenate | solution.py:89
  60.6 3.8 %all-to-all-start.1 = ((bf16[3,2,2,259,256]{4,2,3,0,1:T(2,128)(2,1)}), bf16[3,2,2,259,256]{4,2,3,0,1:T(2,128)(2,1)S(1)}, u32[]{:S(2)}, u32[]{:S(2)}) async-start(bf16[3,2,2,259,256]{4,2,3,0,1:T(2,128)(2,1)} %pad_maximum_fusion), calls=%async_computation.1 | async-start | bytes 3182592 | tf_op jit(solution)/shard_map/all_to_all | solution.py:90
  64.4 0.0 all-reduce.2.cloned.1.call-start
  64.5 0.0 copy-done.8
  64.5 0.1 broadcast_in_dim.50
  64.6 0.2 select_reduce_fusion
  64.8 19.6 %all-to-all-done.1 = bf16[3,2,2,259,256]{4,2,3,0,1:T(2,128)(2,1)S(1)} async-done(((bf16[3,2,2,259,256]{4,2,3,0,1:T(2,128)(2,1)}), bf16[3,2,2,259,256]{4,2,3,0,1:T(2,128)(2,1)S(1)}, u32[]{:S(2)}, u32[]{:S(2)}) %all-to-all-start.1) | async-done | bytes 1591328 | tf_op jit(solution)/shard_map/all_to_all | solution.py:90
  84.4 1.2 copy-done
  85.6 1.6 copy.78
  87.2 0.1 broadcast_in_dim.48
  87.3 4.5 %while.20 = (s32[]{:T(128)}, f32[6,256,256]{2,1,0:T(8,128)S(1)}, f32[6,256]{1,0:T(8,128)S(1)}, bf16[6,2,259,256]{3,2,0,1:T(8,128)(2,1)S(1)}, f32[6]{0:T(128)S(1)}, /*index=5*/s32[]{:T(128)}, s32[]{:T(128)}) while((s32[]{:T(128)}, f32[6,256,256]{2,1,0:T(8,128)S(1)}, f32[6,256]{1,0:T(8,128)S(1)}, ...), condition=%wide.region_2.3_spmd.clone, body=%wide.region_1.2_spmd.clone.sunk | while | flops 1015346944 | bytes 9977029 | solution.py:79
  87.3 0.1 dynamic-slice_bitcast_fusion.2
  87.5 0.1 convert_multiply_fusion.2
  87.5 0.1 multiply_multiply_fusion.3
  87.7 0.1 slice_convert_fusion.7
  87.8 1.4 fusion.60
  89.2 0.3 fusion.61
  89.5 0.1 dynamic_update_slice.20
  89.6 0.1 dynamic-slice_bitcast_fusion.2
  89.7 0.1 convert_multiply_fusion.2
  89.8 0.1 multiply_multiply_fusion.3
  89.9 0.1 slice_convert_fusion.7
  90.1 1.4 fusion.60
  91.4 0.3 fusion.61
  91.8 0.1 dynamic_update_slice.20
  91.9 0.1 constant_dynamic-update-slice_fusion
  92.0 0.1 dynamic-update-slice.5
  92.1 0.1 fusion.42
  92.2 0.3 copy.79
  92.5 1.8 %collective-permute-start = (f32[2,257,256]{2,0,1:T(2,128)S(1)}, f32[2,257,256]{2,0,1:T(2,128)S(1)}, u32[]{:S(2)}, u32[]{:S(2)}) collective-permute-start(f32[2,257,256]{2,0,1:T(2,128)S(1)} %copy.79), channel_id=1, source_target_pairs={{0,4},{4,8},{8,12},{12,16},{16,20},{20,24},{24,28},{28,0},{1,5},{5... | collective-permute-start | bytes 1579016 | tf_op jit(solution)/shard_map/ppermute | solution.py:20
  94.3 0.3 copy.81
  94.6 0.0 copy-start.1
  94.6 3.0 %collective-permute-start.1 = (f32[2,257,256]{2,0,1:T(2,128)S(1)}, f32[2,257,256]{2,0,1:T(2,128)S(1)}, u32[]{:S(2)}, u32[]{:S(2)}) collective-permute-start(f32[2,257,256]{2,0,1:T(2,128)S(1)} %copy.81), channel_id=1, source_target_pairs={{4,0},{8,4},{12,8},{16,12},{20,16},{24,20},{28,24},{0,28},{5,1},{9... | collective-permute-start | bytes 1579016 | tf_op jit(solution)/shard_map/ppermute | solution.py:22
  97.6 12.5 %collective-permute-done = f32[2,257,256]{2,0,1:T(2,128)S(1)} collective-permute-done((f32[2,257,256]{2,0,1:T(2,128)S(1)}, f32[2,257,256]{2,0,1:T(2,128)S(1)}, u32[]{:S(2)}, u32[]{:S(2)}) %collective-permute-start) | collective-permute-done | bytes 526368 | tf_op jit(solution)/shard_map/ppermute | solution.py:20
  110.1 8.2 %collective-permute-done.1 = f32[2,257,256]{2,0,1:T(2,128)S(1)} collective-permute-done((f32[2,257,256]{2,0,1:T(2,128)S(1)}, f32[2,257,256]{2,0,1:T(2,128)S(1)}, u32[]{:S(2)}, u32[]{:S(2)}) %collective-permute-start.1) | collective-permute-done | bytes 526368 | tf_op jit(solution)/shard_map/ppermute | solution.py:22
  118.2 0.1 fusion.18
  118.3 0.0 copy-start.2
  118.3 0.9 slice.97
  119.2 0.0 all-reduce.2.cloned.1.call-update
  119.3 0.0 copy-done.2
  119.3 0.2 copy.72
  119.5 1.5 reshape_squeeze.4
  121.1 0.6 fusion.19
  121.7 0.7 slice.98
  122.5 6.4 %psum.15 = f32[2,256]{1,0:T(2,128)S(1)} all-reduce(f32[2,256]{1,0:T(2,128)S(1)} %bitcast.109), channel_id=1, replica_groups=mesh['tm'=2,'space'=4,'member'=4] {'member'}, use_global_device_ids=true, to_apply=%region_4.5 | all-reduce | flops 512 | bytes 4096 | tf_op jit(solution)/shard_map/psum | solution.py:107
  128.8 23.1 %all-reduce.2.cloned.1.call-done = f32[2,256,256]{2,1,0:T(8,128)} async-done(((f32[2,256,256]{2,1,0:T(8,128)}), f32[2,256,256]{2,1,0:T(8,128)}) %all-reduce.2.cloned.1.call-update) | async-done | bytes 524304 | tf_op jit(solution)/shard_map/psum | solution.py:107
  151.9 2.1 %fusion.24 = f32[2,256,256]{1,2,0:T(8,128)S(1)} fusion(f32[2,256,256]{2,1,0:T(8,128)S(1)} %fusion.19, f32[2,256,256]{2,1,0:T(8,128)} %all-reduce.2.cloned.1.call-done, f32[256,256]{1,0:T(8,128)S(1)} %fusion.30), kind=kOutput, calls=%fused_computation.44 | convolution fusion | flops 402784256 | bytes 1835008 | tf_op jit(solution)/shard_map/tij,tjk->tik/dot_general | solution.py:114
  154.0 0.7 fusion.17
  154.7 1.1 fusion.43
  155.8 0.7 fusion.22
  156.5 1.1 fusion.15
  157.5 0.4 fusion.38
  157.9 0.4 fusion.36
  158.3 0.5 add_convert_fusion
  158.8 1.2 copy.116
  (30 shorter events, 0.2 us)
Async XLA Ops:
  19.4 4.4 %copy-start.4 = (s32[3,2,2,1024]{3,2,1,0:T(2,128)S(1)}, s32[3,2,2,1024]{3,2,1,0:T(2,128)}, u32[]{:S(2)}) copy-start(s32[3,2,2,1024]{3,2,1,0:T(2,128)} %param.21) | copy-start | bytes 147460
  19.4 4.4 %copy-start.5 = (bf16[3,2,2,1024]{3,2,1,0:T(2,128)(2,1)S(1)}, bf16[3,2,2,1024]{3,2,1,0:T(2,128)(2,1)}, u32[]{:S(2)}) copy-start(bf16[3,2,2,1024]{3,2,1,0:T(2,128)(2,1)} %param.20) | copy-start | bytes 73732
  19.4 4.4 %copy-start.6 = (bf16[3,2,2,1024]{3,2,1,0:T(2,128)(2,1)S(1)}, bf16[3,2,2,1024]{3,2,1,0:T(2,128)(2,1)}, u32[]{:S(2)}) copy-start(bf16[3,2,2,1024]{3,2,1,0:T(2,128)(2,1)} %param.19) | copy-start | bytes 73732
  19.4 24.4 %all-to-all-start = ((bf16[4,2,98304]{2,1,0:T(2,128)(2,1)}), bf16[4,2,98304]{2,1,0:T(2,128)(2,1)S(1)}, u32[]{:S(2)}, u32[]{:S(2)}) async-start(bf16[4,2,98304]{2,1,0:T(2,128)(2,1)} %reshape.154), calls=%async_computation | async-start | bytes 3145728 | tf_op jit(solution)/shard_map/all_to_all | solution.py:88
  60.6 3.9 %copy-start.8 = (s32[2,8]{1,0:T(2,128)S(1)}, s32[2,8]{1,0:T(2,128)}, u32[]{:S(2)}) copy-start(s32[2,8]{1,0:T(2,128)} %param.22) | copy-start | bytes 196
  60.6 23.7 %all-to-all-start.1 = ((bf16[3,2,2,259,256]{4,2,3,0,1:T(2,128)(2,1)}), bf16[3,2,2,259,256]{4,2,3,0,1:T(2,128)(2,1)S(1)}, u32[]{:S(2)}, u32[]{:S(2)}) async-start(bf16[3,2,2,259,256]{4,2,3,0,1:T(2,128)(2,1)} %pad_maximum_fusion), calls=%async_computation.1 | async-start | bytes 3182592 | tf_op jit(solution)/shard_map/all_to_all | solution.py:90
  64.4 87.5 %all-reduce.2.cloned.1.call-start = ((), (), s32[]{:S(2)}) async-start(), calls=%async_computation.2 | async-start | bytes 1048576 | tf_op jit(solution)/shard_map/psum | solution.py:107
  84.4 1.2 copy-start
  92.5 17.6 %collective-permute-start = (f32[2,257,256]{2,0,1:T(2,128)S(1)}, f32[2,257,256]{2,0,1:T(2,128)S(1)}, u32[]{:S(2)}, u32[]{:S(2)}) collective-permute-start(f32[2,257,256]{2,0,1:T(2,128)S(1)} %copy.79), channel_id=1, source_target_pairs={{0,4},{4,8},{8,12},{12,16},{16,20},{20,24},{24,28},{28,0},{1,5},{5... | collective-permute-start | bytes 1579016 | tf_op jit(solution)/shard_map/ppermute | solution.py:20
  94.6 24.7 %copy-start.1 = (f32[1,2,256,256]{3,2,1,0:T(8,128)S(1)}, f32[1,2,256,256]{3,2,1,0:T(8,128)}, u32[]{:S(2)}) copy-start(f32[1,2,256,256]{3,2,1,0:T(8,128)} %param.23) | copy-start | bytes 1572868
  94.6 23.6 %collective-permute-start.1 = (f32[2,257,256]{2,0,1:T(2,128)S(1)}, f32[2,257,256]{2,0,1:T(2,128)S(1)}, u32[]{:S(2)}, u32[]{:S(2)}) collective-permute-start(f32[2,257,256]{2,0,1:T(2,128)S(1)} %copy.81), channel_id=1, source_target_pairs={{4,0},{8,4},{12,8},{16,12},{20,16},{24,20},{28,24},{0,28},{5,1},{9... | collective-permute-start | bytes 1579016 | tf_op jit(solution)/shard_map/ppermute | solution.py:22
  118.3 1.0 copy-start.2
  119.3 1.7 %copy-start.7 = (f32[1,2,8,128]{3,2,1,0:T(8,128)S(1)}, f32[1,2,8,128]{3,2,1,0:T(8,128)}, u32[]{:S(2)}) copy-start(f32[1,2,8,128]{3,2,1,0:T(8,128)} %param.25) | copy-start | bytes 24580
  154.0 1.8 %copy-start.3 = (f32[2,256,256]{2,1,0:T(8,128)S(1)}, f32[2,256,256]{2,1,0:T(8,128)}, u32[]{:S(2)}) copy-start(f32[2,256,256]{2,1,0:T(8,128)} %all-reduce.2.cloned.1.call-done) | copy-start | bytes 1572868
Sparse Core Ops, SparseCore 0:
  119.4 32.4 all-reduce.1
where the time goes:
time: 168 us; the launch traced here: 167 us
  waiting for transfers between devices  83.2 us (50%)
  local copies, waits for them, and re-layouts  35.3 us (21%)
  between operations  13.7 us (8%)
  starting transfers between devices  13 us (8%)
  matrix products  10.8 us (6%)
  blocking collectives  6.37 us (4%)
  other arithmetic  4.26 us (3%)
    psum x1, waiting for transfers between devices, body(): gram_sums, proj_sums = lax.psum((gram_sums, proj_sums), 'member')  23.1 us
    unnamed x27, local copies, waits for them, and re-layouts  21.1 us
    all_to_all x1, waiting for transfers between devices, body(): lax.all_to_all(obs_anom, 'member', split_axis=4, concat_axis=3, tiled=True)  19.9 us
    all_to_all x1, waiting for transfers between devices, body(): lax.all_to_all(combined, 'tm', split_axis=1, concat_axis=0, tiled=True)  19.6 us
    ppermute x1, waiting for transfers between devices, with_halo(): lax.ppermute(tail, axis, [(i, (i + 1) % count) for i in range(count)])  12.5 us
    all_to_all x1, local copies, waits for them, and re-layouts, body(): lax.all_to_all(obs_anom, 'member', split_axis=4, concat_axis=3, tiled=True)  9.78 us
    ppermute x1, waiting for transfers between devices, with_halo(): lax.ppermute(head, axis, [((i + 1) % count, i) for i in range(count)])  8.16 us
    psum x1, blocking collectives, body(): gram_sums, proj_sums = lax.psum((gram_sums, proj_sums), 'member')  6.37 us
  transfers between devices with their start and end apart: 5, of which 5 were waited for; matrix products, arithmetic and copies ran while one was open for 2% of the time, Pallas kernels for 0%

commit v1 on v0

v1 whole, which is shorter than its diff:
```python
import functools
import math

import jax
import jax.numpy as jnp
from jax import lax
from jax.experimental import pallas as pl
from jax.experimental.pallas import tpu as pltpu
from jax.sharding import PartitionSpec as P

HALO = 2
NEWTON = 2
WINDOW = 2 * HALO + 1
PAD = 16
MESH = pl.DeviceIdType.MESH
F32 = jnp.float32
BF16 = jnp.bfloat16


def split(x):
    hi = x.astype(BF16)
    return hi, (x - hi.astype(F32)).astype(BF16)


def dot_nn(a, b):
    return jnp.dot(a, b, preferred_element_type=F32)


def dot_nt(a, b):
    return lax.dot_general(a, b, (((1,), (1,)), ((), ())), preferred_element_type=F32)


def dot3(a, b, dot):
    ah, al = a
    bh, bl = b
    return dot(ah, bh) + (dot(ah, bl) + dot(al, bh))


def kernel(
    groups,
    spaces,
    parts,
    columns,
    obs_ref,
    prec_ref,
    innov_ref,
    column_ref,
    cut_ref,
    root_hbm,
    mean_hbm,
    out_ref,
    flat_ref,
    held,
    roots,
    means_in,
    recv,
    prec,
    innov,
    column,
    lhs,
    gram,
    proj,
    square,
    core_out,
    core_in,
    core_proj,
    halo_out,
    halo_in,
    halo_proj_out,
    halo_proj,
    far_out,
    far_in,
    far_proj_out,
    far_proj,
    back_out,
    back_in,
    send_sem,
    recv_sem,
    own_sem,
    local_sem,
    info_sem,
    pair_send,
    pair_recv,
):
    slots, _, tiles, share, obs = obs_ref.shape
    members = share * parts
    quarter = obs // parts
    block = members // 2
    half = block // 2
    extended = tiles + 2 * HALO
    g = lax.axis_index("tm")
    z = lax.axis_index("space")
    m = lax.axis_index("member")
    ring = groups * spaces
    place = g * spaces + z
    right = lax.rem(place + 1, ring)
    left = lax.rem(place + ring - 1, ring)

    def ring_id(index):
        return {"tm": lax.div(index, spaces), "space": lax.rem(index, spaces)}

    peers = [(dt, dm) for dt in range(groups) for dm in range(parts) if dt or dm]
    peers.sort(key=lambda p: (-(p[0] + (p[1] > 0)), p[1]))

    def peer_id(dt, dm):
        return {"tm": lax.rem(g + dt, groups), "member": lax.rem(m + dm, parts)}

    core_bit = lax.rem(m, 2)
    core_id = {"member": m + 1 - 2 * core_bit}
    span = parts // 2
    far_id = {"member": lax.rem(m + span, parts)}

    barrier = pltpu.get_barrier_semaphore()
    for side in (left, right):
        pl.semaphore_signal(barrier, inc=1, device_id=ring_id(side), device_id_type=MESH)
    for dt, dm in peers:
        pl.semaphore_signal(barrier, inc=1, device_id=peer_id(dt, dm), device_id_type=MESH)

    def own_copy(c):
        return pltpu.make_async_copy(
            obs_ref.at[c, g, :, :, pl.ds(pl.multiple_of(m * quarter, quarter), quarter)],
            recv.at[
                c,
                :,
                pl.ds(pl.multiple_of(m * share, share), share),
                pl.ds(pl.multiple_of(g * quarter, quarter), quarter),
            ],
            own_sem.at[c],
        )

    quarter_mine = pl.ds(pl.multiple_of(m * quarter, quarter), quarter)
    quarter_group = pl.ds(pl.multiple_of(g * quarter, quarter), quarter)
    vectors = [(prec_ref, prec), (innov_ref, innov), (column_ref, column)]

    def own_info():
        return [
            pltpu.make_async_copy(
                src.at[:, g, :, quarter_mine], dst.at[:, :, quarter_group], info_sem.at[0, n]
            )
            for n, (src, dst) in enumerate(vectors)
        ]

    def info_copy(dt):
        other = lax.rem(g + dt, groups)
        return [
            pltpu.make_async_remote_copy(
                src_ref=src.at[:, other, :, quarter_mine],
                dst_ref=dst.at[:, :, quarter_group],
                send_sem=info_sem.at[2 * dt - 1, n],
                recv_sem=info_sem.at[2 * dt, n],
                device_id={"tm": other},
                device_id_type=MESH,
            )
            for n, (src, dst) in enumerate(vectors)
        ]

    def obs_copy(c, slot, dt, dm):
        to_m = lax.rem(m + dm, parts)
        return pltpu.make_async_remote_copy(
            src_ref=held.at[
                c,
                lax.rem(g + dt, groups),
                :,
                :,
                pl.ds(pl.multiple_of(to_m * quarter, quarter), quarter),
            ],
            dst_ref=recv.at[
                c,
                :,
                pl.ds(pl.multiple_of(m * share, share), share),
                pl.ds(pl.multiple_of(g * quarter, quarter), quarter),
            ],
            send_sem=send_sem.at[c, slot],
            recv_sem=recv_sem.at[c, slot],
            device_id=peer_id(dt, dm),
            device_id_type=MESH,
        )

    held_copies = [
        pltpu.make_async_copy(obs_ref.at[c], held.at[c], local_sem.at[c]) for c in range(slots)
    ]
    root_copy = pltpu.make_async_copy(root_hbm.at[0], roots, local_sem.at[slots])
    mean_copy = pltpu.make_async_copy(mean_hbm.at[0], means_in, local_sem.at[slots + 1])
    for copy in held_copies:
        copy.start()
    for copy in own_info():
        copy.start()
    root_copy.start()
    mean_copy.start()
    for c in range(slots):
        own_copy(c).start()
    pl.semaphore_wait(barrier, len(peers) + 2)
    for dt in range(1, groups):
        for copy in info_copy(dt):
            copy.start()
    for c in range(slots):
        held_copies[c].wait()
        for slot, (dt, dm) in enumerate(peers):
            obs_copy(c, slot, dt, dm).start()

    gram[...] = jnp.zeros_like(gram)
    proj[...] = jnp.zeros_like(proj)
    root_copy.wait()
    mean_copy.wait()
    levels = means_in.shape[1]
    for t in range(tiles):
        for level in range(levels):
            flat_ref[t : t + 1, level * columns : (level + 1) * columns] = means_in[
                t, level : level + 1
            ]
        x = split(roots[t])
        square[t] = dot3(x, x, dot_nn)

    per_sector = cut_ref.shape[1]
    cycle = cut_ref.shape[0] * per_sector
    first = place * tiles
    reaches = []
    for e in range(extended):
        at = lax.rem(first + e - HALO + cycle, cycle)
        reach = cut_ref[lax.div(at, per_sector), lax.rem(at, per_sector)]
        reaches.append((reach.astype(F32) + 0.5) * columns)

    for copy in own_info():
        copy.wait()
    for dt in range(1, groups):
        for copy in info_copy(dt):
            copy.wait()

    wide = groups * quarter
    row = lax.broadcasted_iota(jnp.int32, (PAD, wide), 0)
    shift = (HALO - row).astype(F32) * columns

    def add_chunk(c, carry):
        own_copy(c).wait()
        for slot, (dt, dm) in enumerate(peers):
            obs_copy(c, slot, dt, dm).wait_recv()
        all_precision = prec[c].astype(F32)
        all_innovation = innov[c].astype(F32)
        all_placing = column[c].astype(F32) + (0.5 - columns / 2)
        for u in range(tiles):
            precision = all_precision[u : u + 1]
            innovation = all_innovation[u : u + 1]
            placing = all_placing[u : u + 1]
            reach = jnp.ones((PAD, wide), F32)
            for w in range(WINDOW):
                reach = jnp.where(row == w, reaches[u + w], reach)
            relative = (shift + placing) / reach
            taper = jnp.square(jnp.maximum(1.0 - relative * relative, 0.0))
            coeffs = jnp.where(row < WINDOW, taper * precision, 0.0)
            anomaly = recv[c, u]
            wide_anomaly = anomaly.astype(F32)
            for w in range(WINDOW):
                lhs[w * members : (w + 1) * members] = (
                    wide_anomaly * coeffs[w : w + 1]
                ).astype(BF16)
            lhs[WINDOW * members :] = (coeffs * innovation).astype(BF16)
            sums = dot_nt(lhs[...], anomaly)
            for w in range(WINDOW):
                gram[u + w] += sums[w * members : (w + 1) * members]
            base = WINDOW * members
            proj[u : u + WINDOW, :members] += sums[base : base + WINDOW]
        return carry

    lax.fori_loop(0, slots, add_chunk, 0)

    def remote(src, dst, index, target):
        return pltpu.make_async_remote_copy(
            src_ref=src,
            dst_ref=dst,
            send_sem=pair_send.at[index],
            recv_sem=pair_recv.at[index],
            device_id=target,
            device_id_type=MESH,
        )

    rows = lax.broadcasted_iota(jnp.int32, (block, block), 0)
    cols = lax.broadcasted_iota(jnp.int32, (block, block), 1)
    for e in range(extended):
        corner = gram[e, block:, block:]
        diagonal = jnp.sum(jnp.where(rows == cols, corner, 0.0), axis=0, keepdims=True)
        proj[e : e + 1, members:] = diagonal
        gram[e, :block, :block] = jnp.where(rows <= cols, gram[e, :block, :block], corner)

    mine = pl.multiple_of(core_bit * half, half)
    theirs = pl.multiple_of((1 - core_bit) * half, half)

    core_out[...] = gram[:, pl.ds(theirs, half)].astype(BF16)
    core_copies = [
        remote(core_out, core_in, 0, core_id),
        remote(proj, core_proj, 1, core_id),
    ]
    for copy in core_copies:
        copy.start()
    for copy in core_copies:
        copy.wait()

    summed = proj[...] + core_proj[...]
    halo_proj_out[...] = jnp.zeros_like(halo_proj_out)
    far_proj_out[...] = jnp.zeros_like(far_proj_out)
    pieces_of = summed.shape[1] // block

    def pack(target, first_row, count):
        for h in range(count):
            for k in range(pieces_of):
                at = h * pieces_of + k
                target[at : at + 1] = summed[
                    first_row + h : first_row + h + 1, k * block : (k + 1) * block
                ]

    pack(halo_proj_out.at[0], 0, HALO)
    pack(halo_proj_out.at[1], tiles + HALO, HALO)
    pack(far_proj_out, HALO, tiles)
    low = gram[:HALO, pl.ds(mine, half)] + core_in[:HALO].astype(F32)
    halo_out[0] = low.astype(BF16)
    high = gram[tiles + HALO :, pl.ds(mine, half)] + core_in[tiles + HALO :].astype(F32)
    halo_out[1] = high.astype(BF16)
    halo_copies = [
        remote(halo_out.at[0], halo_in.at[0], 2, ring_id(left)),
        remote(halo_out.at[1], halo_in.at[1], 3, ring_id(right)),
        remote(halo_proj_out.at[0], halo_proj.at[0], 4, ring_id(left)),
        remote(halo_proj_out.at[1], halo_proj.at[1], 5, ring_id(right)),
    ]
    for copy in halo_copies:
        copy.start()
    owned = [
        gram[HALO + t, pl.ds(mine, half)] + core_in[HALO + t].astype(F32) for t in range(tiles)
    ]
    for copy in halo_copies:
        copy.wait()
    strip = HALO * pieces_of
    start = (tiles - HALO) * pieces_of
    far_proj_out[:strip] += halo_proj[1, :strip]
    far_proj_out[start : start + strip] += halo_proj[0, :strip]
    for h in range(HALO):
        owned[h] = owned[h] + halo_in[1, h].astype(F32)
        t = tiles - HALO + h
        owned[t] = owned[t] + halo_in[0, h].astype(F32)

    for t in range(tiles):
        far_out[t] = owned[t].astype(BF16)
        gram[t, pl.ds(mine, half)] = owned[t]
    far_copies = [
        remote(far_out, far_in, 6, far_id),
        remote(far_proj_out, far_proj, 7, far_id),
    ]
    for copy in far_copies:
        copy.start()
    for copy in far_copies:
        copy.wait()

    for t in range(tiles):
        total = gram[t, pl.ds(mine, half)] + far_in[t].astype(F32)
        gram[t, pl.ds(mine, half)] = total
        back_out[t] = total.astype(BF16)
    back_copy = remote(back_out, back_in, 8, core_id)
    back_copy.start()
    back_copy.wait()
    for t in range(tiles):
        gram[t, pl.ds(theirs, half)] = back_in[t].astype(F32)

    packed_proj = far_proj_out[...] + far_proj[...]
    for t in range(tiles):
        for k in range(pieces_of):
            at = t * pieces_of + k
            proj[t : t + 1, k * block : (k + 1) * block] = packed_proj[at : at + 1]
    total_proj = proj[...]
    inflation = members - 1.0
    eye = jnp.where(
        lax.broadcasted_iota(jnp.int32, (members, members), 0)
        == lax.broadcasted_iota(jnp.int32, (members, members), 1),
        1.0,
        0.0,
    )
    systems = []
    for t in range(tiles):
        packed = gram[t, :block, :block]
        flipped = packed.T
        cross = gram[t, :block, block:]
        gram[t, :block, :block] = jnp.where(rows <= cols, packed, flipped)
        corner = jnp.where(rows > cols, packed, flipped)
        gram[t, block:, block:] = jnp.where(rows == cols, total_proj[t : t + 1, members:], corner)
        gram[t, block:, :block] = cross.T
        systems.append(split(gram[t] + inflation * eye))
    xs = [roots[t] for t in range(tiles)]
    for step in range(NEWTON):
        pieces = [split(x) for x in xs]
        if step == 0:
            powers = [square[t] for t in range(tiles)]
        else:
            powers = [dot3(piece, piece, dot_nn) for piece in pieces]
        powers = [split(power) for power in powers]
        applied = [dot3(system, power, dot_nn) for system, power in zip(systems, powers)]
        excess = [(a - eye).astype(BF16) for a in applied]
        xs = [x - 0.5 * dot_nn(piece[0], d) for x, piece, d in zip(xs, pieces, excess)]
    pieces = [split(x) for x in xs]
    totals = split(total_proj[:, :members])
    inner = [dot3(piece, totals, dot_nt) for piece in pieces]
    means = [dot3(piece, split(part), dot_nn) for piece, part in zip(pieces, inner)]
    for t in range(tiles):
        out_ref[t] = (means[t][:, t : t + 1] + math.sqrt(inflation) * xs[t]).astype(BF16)

    def drain(c, carry):
        for slot, (dt, dm) in enumerate(peers):
            obs_copy(c, slot, dt, dm).wait_send()
        return carry

    lax.fori_loop(0, slots, drain, 0)


def body(mesh_shape, obs_anom, obs_prec, innov, obs_column, cutoff, inv_root, state_anom, state_mean):
    groups, spaces, parts = (mesh_shape[name] for name in ("tm", "space", "member"))
    slots, _, tiles, share, obs = obs_anom.shape
    columns = state_anom.shape[-1]
    members = share * parts
    quarter = obs // parts
    half = members // 4
    long = members + members // 2
    extended = tiles + 2 * HALO
    halo_rows = -(-3 * HALO // 8) * 8
    far_rows = -(-3 * tiles // 8) * 8
    vmem = pl.BlockSpec(memory_space=pltpu.VMEM)
    hbm = pl.BlockSpec(memory_space=pl.ANY)
    peers = groups * parts - 1
    levels = state_mean.shape[2]
    weights, flat = pl.pallas_call(
        functools.partial(kernel, groups, spaces, parts, columns),
        out_shape=[
            jax.ShapeDtypeStruct((tiles, members, members), BF16),
            jax.ShapeDtypeStruct((tiles, levels * columns), F32),
        ],
        in_specs=[hbm, hbm, hbm, hbm, pl.BlockSpec(memory_space=pltpu.SMEM), hbm, hbm],
        out_specs=[vmem, vmem],
        scratch_shapes=[
            pltpu.VMEM(obs_anom.shape, BF16),
            pltpu.VMEM((tiles, members, members), F32),
            pltpu.VMEM((tiles, levels, columns), F32),
            pltpu.VMEM((slots, tiles, members, groups * quarter), BF16),
            pltpu.VMEM((slots, tiles, groups * quarter), BF16),
            pltpu.VMEM((slots, tiles, groups * quarter), BF16),
            pltpu.VMEM((slots, tiles, groups * quarter), jnp.int32),
            pltpu.VMEM((WINDOW * members + PAD, groups * quarter), BF16),
            pltpu.VMEM((extended, members, members), F32),
            pltpu.VMEM((8, long), F32),
            pltpu.VMEM((tiles, members, members), F32),
            pltpu.VMEM((extended, half, members), BF16),
            pltpu.VMEM((extended, half, members), BF16),
            pltpu.VMEM((8, long), F32),
            pltpu.VMEM((2, HALO, half, members), BF16),
            pltpu.VMEM((2, HALO, half, members), BF16),
            pltpu.VMEM((2, halo_rows, members // 2), F32),
            pltpu.VMEM((2, halo_rows, members // 2), F32),
            pltpu.VMEM((tiles, half, members), BF16),
            pltpu.VMEM((tiles, half, members), BF16),
            pltpu.VMEM((far_rows, members // 2), F32),
            pltpu.VMEM((far_rows, members // 2), F32),
            pltpu.VMEM((tiles, half, members), BF16),
            pltpu.VMEM((tiles, half, members), BF16),
            pltpu.SemaphoreType.DMA((slots, peers)),
            pltpu.SemaphoreType.DMA((slots, peers)),
            pltpu.SemaphoreType.DMA((slots,)),
            pltpu.SemaphoreType.DMA((slots + 2,)),
            pltpu.SemaphoreType.DMA((2 * groups - 1, 3)),
            pltpu.SemaphoreType.DMA((9,)),
            pltpu.SemaphoreType.DMA((9,)),
        ],
        compiler_params=pltpu.CompilerParams(collective_id=0, has_side_effects=True),
    )(obs_anom, obs_prec, innov, obs_column, cutoff, inv_root, state_mean)
    anomalies = state_anom[0].reshape(tiles, members, -1)
    mean_rows = flat[:, None, :]
    result = (
        jnp.einsum("tij,tiq->tjq", weights, anomalies, preferred_element_type=F32) + mean_rows
    )
    return result.astype(BF16).reshape(state_anom.shape)


def solution(mesh):
    in_specs = (
        P("tm", None, "space", "member", None),
        P("tm", None, "space", None),
        P("tm", None, "space", None),
        P("tm", None, "space", None),
        P(),
        P("tm", "space", None, None),
        P("tm", "space", None, "member", None),
        P("tm", "space", "member", None),
    )
    out_specs = P("tm", "space", None, "member", None)
    step = functools.partial(body, dict(mesh.shape))
    return jax.shard_map(step, mesh=mesh, in_specs=in_specs, out_specs=out_specs, check_vma=False)
```

time: 168 us -> 44.7 us (0.27)
  waiting for transfers between devices: 83.2 us -> 0 us
  Pallas kernels: 0 us -> 41.9 us
  local copies, waits for them, and re-layouts: 35.3 us -> 2.17 us
  between operations: 13.7 us -> 0.05 us
  starting transfers between devices: 13 us -> 0 us
  matrix products: 10.8 us -> 0.49 us
  blocking collectives: 6.37 us -> 0 us
  other arithmetic: 4.26 us -> 0 us
    pallas_call x0 -> x1, Pallas kernels: none -> 41.9 us  [body(): pl.pallas_call(functools.partial(kernel, groups, spaces, parts, columns),...]
    all_to_all x2 -> x0, waiting for transfers between devices: 39.5 us -> none  [the longest x1 19.9 us: body(): lax.all_to_all(obs_anom, 'member', split_axis=4, concat_axis=3, tiled=True)]
    psum x1 -> x0, waiting for transfers between devices: 23.1 us -> none  [body(): gram_sums, proj_sums = lax.psum((gram_sums, proj_sums), 'member')]
    ppermute x2 -> x0, waiting for transfers between devices: 20.6 us -> none  [the longest x1 12.5 us: with_halo(): lax.ppermute(tail, axis, [(i, (i + 1) % count) for i in range(count)])]
    unnamed x27 -> x7, local copies, waits for them, and re-layouts: 21.1 us -> 1.68 us
    dot_general x13 -> x1, matrix products: 10.8 us -> 0.49 us  [body(): jnp.einsum('tij,tiq->tjq', weights, anomalies, preferred_element_type=F32)]
    all_to_all x1 -> x0, local copies, waits for them, and re-layouts: 9.78 us -> none  [body(): lax.all_to_all(obs_anom, 'member', split_axis=4, concat_axis=3, tiled=True)]
    all_to_all x2 -> x0, starting transfers between devices: 8.18 us -> none  [the longest x1 4.37 us: body(): lax.all_to_all(obs_anom, 'member', split_axis=4, concat_axis=3, tiled=True)]
  transfers between devices with their start and end apart: 5 -> 0, of which waited for: 5 -> 0; matrix products, arithmetic and copies ran while one was open for 2% -> 0% of each run, Pallas kernels for 0% -> 0%
where the time goes in v1:
time: 44.7 us; the launch traced here: 44.6 us
  Pallas kernels  41.9 us (94%)
  local copies, waits for them, and re-layouts  2.17 us (5%)
  matrix products  0.49 us (1%)
    pallas_call x1, Pallas kernels, body(): pl.pallas_call(functools.partial(kernel, groups, spaces, parts, columns),...  41.9 us
    unnamed x7, local copies, waits for them, and re-layouts  1.68 us

profile of v1, /device:TPU:0, one launch (start us, length us, event | category | flops | bytes accessed | tf_op | source)
XLA Modules:
  0.0 44.6 jit_solution(4205220312761842819)
XLA Ops:
  0.0 0.0 copy-start
  0.0 41.9 %shard_map.82 = (bf16[2,256,256]{2,1,0:T(8,128)(2,1)}, f32[2,1024]{1,0:T(2,128)}) custom-call(bf16[3,2,2,64,1024]{4,3,2,1,0:T(8,128)(2,1)} %obs_ref.1, bf16[3,2,2,1024]{3,2,1,0:T(2,128)(2,1)} %prec_ref.1, bf16[3,2,2,1024]{3,2,1,0:T(2,128)(2,1)} %innov_ref.1, s32[3,2,2,1024]{3,2,1,0:T(2,128)} %column_ref.1, s32[2,8]{1,0:T(2,128)} %cut_ref.1, ...), custom_call_target="tpu_custom_call" | custom-call | tf_op jit(solution)/shard_map/pallas_call | solution.py:425
  41.9 0.0 copy-start.1
  41.9 0.0 copy-start.2
  41.9 0.0 copy-done
  41.9 0.5 %reshape_squeeze.3 = bf16[2,256,1024]{2,1,0:T(8,128)(2,1)S(1)} reshape(bf16[1,2,256,8,128]{4,3,2,1,0:T(8,128)(2,1)S(1)} %copy-done) | data formatting | bytes 2097152 | tf_op jit(solution)/shard_map/reshape;squeeze | solution.py:468
  42.4 0.4 copy-done.1
  42.8 0.0 copy-done.2
  42.8 0.5 %add_convert_fusion = bf16[2,256,1024]{2,1,0:T(8,128)(2,1)S(1)} fusion(bf16[2,256,256]{2,1,0:T(8,128)(2,1)S(1)} %copy-done.1, bf16[2,256,1024]{2,1,0:T(8,128)(2,1)S(1)} %reshape_squeeze.3, f32[2,1024]{1,0:T(2,128)S(1)} %copy-done.2), kind=kOutput, calls=%fused_computation | convolution fusion | flops 269484032 | bytes 2367488 | tf_op jit(solution)/shard_map/tij,tiq->tjq/dot_general | solution.py:471
  43.3 1.2 %copy.11 = bf16[64,8,8,128]{3,2,1,0:T(8,128)(2,1)} copy(bf16[64,8,8,128]{3,1,2,0:T(8,128)(2,1)S(1)} %bitcast.8) | data formatting | bytes 2097152
Async XLA Ops:
  0.0 41.9 %copy-start = (bf16[1,2,256,8,128]{4,3,2,1,0:T(8,128)(2,1)S(1)}, bf16[1,2,256,8,128]{4,3,2,1,0:T(8,128)(2,1)}, u32[]{:S(2)}) copy-start(bf16[1,2,256,8,128]{4,3,2,1,0:T(8,128)(2,1)} %param.14) | copy-start | bytes 3145732
  41.9 1.0 %copy-start.1 = (bf16[2,256,256]{2,1,0:T(8,128)(2,1)S(1)}, bf16[2,256,256]{2,1,0:T(8,128)(2,1)}, u32[]{:S(2)}) copy-start(bf16[2,256,256]{2,1,0:T(8,128)(2,1)} %get-tuple-element.7) | copy-start | bytes 786436
  41.9 0.9 %copy-start.2 = (f32[2,1024]{1,0:T(2,128)S(1)}, f32[2,1024]{1,0:T(2,128)}, u32[]{:S(2)}) copy-start(f32[2,1024]{1,0:T(2,128)} %get-tuple-element.8) | copy-start | bytes 24580
